TPU v7x, 256 devices: a whole 4x4x8 slice. The times are simulated.
256 devices in a mesh: trial: 4 (over z_lo), ep: 4 (over y), fsdp: 16 (over z_hi, x, core).
Axes of the slice: x: 4, y: 4, z: 8 (z_hi: 2, z_lo: 4; z = z_hi * 4 + z_lo), core: 2. Of those that a mesh axis runs over, the one named last changes fastest.
Arguments:
- master_down: float32 [256, 1024, 2048], P(('trial', 'ep'), None, 'fsdp'), parts along dimension 0, may hold values from -0.25 to 0.25
- router_weight: float32 [8192, 64], P(('trial', 'fsdp'), 'ep'), parts along dimension 0, may hold values from -0.125 to 0.125
- router_gain: float32 [8192], P(('trial', 'fsdp')), parts along dimension 0, may hold values from 0.25 to 1.75
Outputs:
- final_down: bfloat16 [256, 1024, 2048], P(('trial', 'ep'), 'fsdp'), parts along dimension 0
- scale_down: float32 [256, 1024], P(('trial', 'ep'), 'fsdp'), parts along dimension 0
- serve_router: bfloat16 [8192, 64], P('trial'), parts along dimension 0
There are 4 independent parts, one for each index of `trial`. A program takes and returns all parts, laid end to end along the dimension named above; each array names one. Nothing has to cross between parts.
All inputs are finite; a program needn't handle non-finite values. Where the computation divides by a largest or mean magnitude, that divisor is 1e-20 or more.
Results may differ from a plain program's by a relative error of at most 0.001.
Values may be sent and summed in bfloat16 or wider, within the bound.
A program may use at most 64 MiB of HBM per device.

v0:
```python
import jax
import jax.numpy as jnp
from jax import lax
from jax.sharding import PartitionSpec as P


def copy_for_each(shard, axis):
    copies = jnp.broadcast_to(shard, (lax.axis_size(axis), *shard.shape))
    return lax.all_to_all(copies, axis, split_axis=0, concat_axis=0, tiled=True)


def taken_together(shard, axis):
    return copy_for_each(shard, axis).max(axis=0)


def laid_out(blocks, dim):
    lengths = list(blocks.shape[1:])
    lengths[dim] *= blocks.shape[0]
    return jnp.moveaxis(blocks, 0, dim).reshape(lengths)


def gathered_copies(shard, axis, dim):
    blocks = copy_for_each(shard, axis)
    return laid_out(blocks, dim)


def shards(master_down, router_weight, router_gain):
    scale_down = taken_together(jnp.max(jnp.abs(master_down), axis=2), "fsdp")
    narrow_down = (master_down / jnp.expand_dims(scale_down, 2)).astype(jnp.bfloat16)
    final_down = lax.all_to_all(narrow_down, "fsdp", split_axis=1, concat_axis=2, tiled=True)
    scale_down = lax.dynamic_slice_in_dim(
        scale_down, lax.axis_index("fsdp") * final_down.shape[1], final_down.shape[1], axis=1
    )
    part_router = (router_weight * router_gain[:, None]).astype(jnp.bfloat16)
    row_router = gathered_copies(part_router, "fsdp", 0)
    serve_router = lax.all_gather(row_router, "ep", axis=1, tiled=True)
    return (final_down, scale_down, serve_router)


def solution(mesh):
    return jax.shard_map(
        shards,
        mesh=mesh,
        in_specs=(
            P(("trial", "ep"), None, "fsdp"),
            P(("trial", "fsdp"), "ep"),
            P(("trial", "fsdp")),
        ),
        out_specs=(P(("trial", "ep"), "fsdp", None), P(("trial", "ep"), "fsdp"), P("trial", None)),
        check_vma=False,
    )
```

profile of v0, /device:TPU:55, one launch (start us, length us, event | category | flops | bytes accessed | tf_op | source)
XLA Modules:
  0.0 194.5 jit_solution(12414777083532193542)
XLA Ops:
  0.6 0.0 copy-start
  0.6 0.0 copy-start.1
  0.7 5.6 %abs_reduce_fusion = f32[16,1024]{1,0:T(8,128)S(1)} fusion(f32[16,1024,128]{2,1,0:T(8,128)} %param.3), kind=kLoop, calls=%fused_computation.2 | loop fusion | flops 4177920 | bytes 8454144 | tf_op jit(solution)/shard_map/reduce_max | solution.py:28
  6.3 1.1 broadcast_in_dim.8
  7.4 10.8 %all-to-all-start = ((f32[16,16,1024]{2,1,0:T(8,128)}), f32[16,16,1024]{2,1,0:T(8,128)S(1)}, u32[]{:S(2)}, u32[]{:S(2)}) async-start(f32[16,16,1024]{2,1,0:T(8,128)} %broadcast_in_dim.8), calls=%async_computation | async-start | bytes 2097152 | tf_op jit(solution)/shard_map/all_to_all | solution.py:9
  18.2 0.0 copy-done
  18.2 0.0 copy-done.1
  18.2 30.0 %all-to-all-done = f32[16,16,1024]{2,1,0:T(8,128)S(1)} async-done(((f32[16,16,1024]{2,1,0:T(8,128)}), f32[16,16,1024]{2,1,0:T(8,128)S(1)}, u32[]{:S(2)}, u32[]{:S(2)}) %all-to-all-start) | async-done | bytes 1048608 | tf_op jit(solution)/shard_map/all_to_all | solution.py:9
  48.2 0.6 broadcast_in_dim.9
  48.8 5.0 %all-to-all-start.2 = ((bf16[16,128,16]{1,2,0:T(8,128)(2,1)}), bf16[16,128,16]{1,2,0:T(8,128)(2,1)S(1)}, u32[]{:S(2)}, u32[]{:S(2)}) async-start(bf16[16,128,16]{1,2,0:T(8,128)(2,1)} %broadcast_in_dim.9), calls=%async_computation.2 | async-start | bytes 131072 | tf_op jit(solution)/shard_map/all_to_all | solution.py:9
  53.8 0.1 reduce_max.19
  53.9 0.2 copy.14
  54.1 9.6 %fusion = bf16[16,1024,128]{2,0,1:T(8,128)(2,1)} fusion(f32[16,1024,128]{2,1,0:T(8,128)} %param.3, f32[16,1024]{0,1:T(8,128)S(1)} %copy.14), kind=kLoop, calls=%fused_computation.1 | loop fusion | flops 4194304 | bytes 12648448 | tf_op jit(solution)/shard_map/convert_element_type | solution.py:29
  63.7 0.0 all-to-all-done.2
  63.7 9.7 %all-to-all-start.1 = ((bf16[16,1024,128]{2,0,1:T(8,128)(2,1)}), bf16[16,1024,128]{2,0,1:T(8,128)(2,1)}, u32[]{:S(2)}, u32[]{:S(2)}) async-start(bf16[16,1024,128]{2,0,1:T(8,128)(2,1)} %fusion), calls=%async_computation.1 | async-start | bytes 8388608 | tf_op jit(solution)/shard_map/all_to_all | solution.py:30
  73.4 9.4 %all_gather.3 = bf16[2048,64]{0,1:T(8,128)(2,1)S(1)} all-gather(bf16[2048,16]{0,1:T(8,128)(2,1)S(1)} %copy_bitcast_fusion), channel_id=1, replica_groups=mesh['trial'=4,'ep'=4,'fsdp'=16] {'ep'}, dimensions={1}, use_global_device_ids=true | all-gather | bytes 327680 | tf_op jit(solution)/shard_map/all_gather | solution.py:36
  82.7 0.7 constant_dynamic-slice_fusion
  83.4 96.2 %all-to-all-done.1 = bf16[16,1024,128]{2,0,1:T(8,128)(2,1)} async-done(((bf16[16,1024,128]{2,0,1:T(8,128)(2,1)}), bf16[16,1024,128]{2,0,1:T(8,128)(2,1)}, u32[]{:S(2)}, u32[]{:S(2)}) %all-to-all-start.1) | async-done | bytes 4194336 | tf_op jit(solution)/shard_map/all_to_all | solution.py:30
  179.7 6.9 %copy.16 = bf16[16,64,16,128]{3,2,1,0:T(8,128)(2,1)} copy(bf16[16,64,16,128]{3,0,1,2:T(8,128)(2,1)} %bitcast.1) | data formatting | bytes 8388608 | tf_op jit(solution)/shard_map/all_to_all | solution.py:30
  186.5 7.3 %all_to_all.23 = bf16[16,64,2048]{2,1,0:T(8,128)(2,1)} reshape(bf16[16,64,16,128]{3,2,1,0:T(8,128)(2,1)} %copy.16) | data formatting | bytes 8388608 | tf_op jit(solution)/shard_map/all_to_all | solution.py:30
  193.8 0.7 copy.24
  (2 shorter events, 0.0 us)
Async XLA Ops:
  0.6 17.5 %copy-start = (f32[128,16]{0,1:T(8,128)S(1)}, f32[128,16]{0,1:T(8,128)}, u32[]{:S(2)}) copy-start(f32[128,16]{0,1:T(8,128)} %param.4) | copy-start | bytes 24580
  0.6 17.5 %copy-start.1 = (f32[128]{0:T(128)S(1)}, f32[128]{0:T(128)}, u32[]{:S(2)}) copy-start(f32[128]{0:T(128)} %param.5) | copy-start | bytes 1540
  7.4 40.8 %all-to-all-start = ((f32[16,16,1024]{2,1,0:T(8,128)}), f32[16,16,1024]{2,1,0:T(8,128)S(1)}, u32[]{:S(2)}, u32[]{:S(2)}) async-start(f32[16,16,1024]{2,1,0:T(8,128)} %broadcast_in_dim.8), calls=%async_computation | async-start | bytes 2097152 | tf_op jit(solution)/shard_map/all_to_all | solution.py:9
  48.8 14.9 %all-to-all-start.2 = ((bf16[16,128,16]{1,2,0:T(8,128)(2,1)}), bf16[16,128,16]{1,2,0:T(8,128)(2,1)S(1)}, u32[]{:S(2)}, u32[]{:S(2)}) async-start(bf16[16,128,16]{1,2,0:T(8,128)(2,1)} %broadcast_in_dim.9), calls=%async_computation.2 | async-start | bytes 131072 | tf_op jit(solution)/shard_map/all_to_all | solution.py:9
  63.7 115.9 %all-to-all-start.1 = ((bf16[16,1024,128]{2,0,1:T(8,128)(2,1)}), bf16[16,1024,128]{2,0,1:T(8,128)(2,1)}, u32[]{:S(2)}, u32[]{:S(2)}) async-start(bf16[16,1024,128]{2,0,1:T(8,128)(2,1)} %fusion), calls=%async_computation.1 | async-start | bytes 8388608 | tf_op jit(solution)/shard_map/all_to_all | solution.py:30
where the time goes:
time: 195 us; the launch traced here: 194 us
  waiting for transfers between devices  126 us (65%)
  starting transfers between devices  25.5 us (13%)
  local copies, waits for them, and re-layouts  17.4 us (9%)
  other arithmetic  15.3 us (8%)
  blocking collectives  9.36 us (5%)
    all_to_all x1, waiting for transfers between devices, shards(): lax.all_to_all(narrow_down, 'fsdp', split_axis=1, concat_axis=2, tiled=True)  96.2 us
    all_to_all x2, waiting for transfers between devices, copy_for_each(): return lax.all_to_all(copies, axis, split_axis=0, concat_axis=0, tiled=True)  30 us
    all_to_all x2, starting transfers between devices, copy_for_each(): return lax.all_to_all(copies, axis, split_axis=0, concat_axis=0, tiled=True)  15.8 us
    all_to_all x2, local copies, waits for them, and re-layouts, shards(): lax.all_to_all(narrow_down, 'fsdp', split_axis=1, concat_axis=2, tiled=True)  14.1 us
    all_to_all x1, starting transfers between devices, shards(): lax.all_to_all(narrow_down, 'fsdp', split_axis=1, concat_axis=2, tiled=True)  9.66 us
    convert_element_type x1, other arithmetic, shards(): (master_down / jnp.expand_dims(scale_down, 2)).astype(jnp.bfloat16)  9.63 us
    all_gather x1, blocking collectives, shards(): serve_router = lax.all_gather(row_router, 'ep', axis=1, tiled=True)  9.36 us
    reduce_max x1, other arithmetic, shards(): scale_down = taken_together(jnp.max(jnp.abs(master_down), axis=2), 'fsdp')  5.62 us
  transfers between devices with their start and end apart: 3, of which 2 were waited for; matrix products, arithmetic and copies ran while one was open for 5% of the time, Pallas kernels for 0%

commit v1 on v0

v1 whole, which is shorter than its diff:
```python
import functools

import jax
import jax.numpy as jnp
from jax import lax
from jax.experimental import pallas as pl
from jax.experimental.pallas import tpu as pltpu
from jax.sharding import PartitionSpec as P

MESH = pl.DeviceIdType.MESH

OFFSETS = [(1, dx, dc) for dx in (0, 1, 3, 2) for dc in (0, 1)] + [
    (0, dx, dc) for dx in (1, 3, 2, 0) for dc in (0, 1) if (dx, dc) != (0, 0)
]
SAME_CORE = [o for o in OFFSETS if o[2] == 0]
FIRST = 2
STEP = 2


def kernel(
    experts,
    rows,
    w_hbm,
    rt_ref,
    gain_ref,
    final_ref,
    scale_ref,
    router_ref,
    w,
    narrow,
    maxima,
    straight,
    paired,
    partner,
    others,
    scales,
    own_router,
    load_sem,
    send_sem,
    recv_sem,
    straight_send,
    straight_recv,
    pair_send,
    pair_recv,
    other_send,
    other_recv,
    back_send,
    back_recv,
    router_send,
    router_recv,
):
    trial, ep, me = lax.axis_index("trial"), lax.axis_index("ep"), lax.axis_index("fsdp")
    plane, x, core = me // 8, lax.rem(me // 2, 4), lax.rem(me, 2)
    share = rows // 16

    def at(offset, sign=1):
        dz, dx, dc = offset
        return lax.rem(plane + dz, 2) * 8 + lax.rem(x + 4 + sign * dx, 4) * 2 + lax.rem(core + dc, 2)

    def send(src, dst, send, recv, index, row=None):
        return pltpu.make_async_remote_copy(
            src_ref=src,
            dst_ref=dst,
            send_sem=send,
            recv_sem=recv,
            device_id=(trial, ep if row is None else row, index),
            device_id_type=MESH,
        )

    def columns(index):
        return pl.ds(pl.multiple_of(index * 128, 128), 128)

    loads = [pltpu.make_async_copy(w_hbm.at[e], w.at[e], load_sem.at[e]) for e in range(experts)]
    for load in loads:
        load.start()

    barrier = pltpu.get_barrier_semaphore()
    for o in OFFSETS:
        pl.semaphore_signal(barrier, inc=1, device_id=(trial, ep, at(o)), device_id_type=MESH)
    for d in (1, 2, 3):
        pl.semaphore_signal(barrier, inc=1, device_id=(trial, lax.rem(ep + d, 4), me), device_id_type=MESH)

    part = (rt_ref[...] * gain_ref[...]).astype(jnp.bfloat16)
    own_router[...] = part
    own_rows = pl.ds(pl.multiple_of(ep * 16, 16), 16)
    router_ref[own_rows, columns(me)] = part

    def take_maxima(e):
        for b in range(rows // 128):
            block = jnp.abs(w[e, b * 128 : (b + 1) * 128, :])
            maxima[e, b : b + 1, :] = jnp.max(block.T, axis=0, keepdims=True)

    def divide(e):
        inverse = 1.0 / scales[e]
        for b in range(rows // 128):
            factor = jnp.broadcast_to(inverse[b : b + 1, :], (128, 128)).T
            narrow[e, b * 128 : (b + 1) * 128, :] = (w[e, b * 128 : (b + 1) * 128, :] * factor).astype(jnp.bfloat16)

    for e in range(FIRST):
        loads[e].wait()
        take_maxima(e)
    pl.semaphore_wait(barrier, len(OFFSETS) + 3)

    straights = [
        send(maxima.at[pl.ds(0, FIRST)], straight.at[i], straight_send.at[i], straight_recv.at[i], at(o))
        for i, o in enumerate(OFFSETS)
    ]
    for s in straights:
        s.start()
    router_y = [
        send(own_router, router_ref.at[own_rows, columns(me)], router_send.at[d - 1], router_recv.at[d - 1], me, lax.rem(ep + d, 4))
        for d in (1, 2, 3)
    ]
    for s in router_y:
        s.start()

    half = (experts - FIRST) // 2
    mine = pl.ds(FIRST + core * half, half)
    theirs = pl.ds(FIRST + (1 - core) * half, half)
    for e in range(FIRST, experts):
        loads[e].wait()

    def later_maxima(e, carry):
        take_maxima(e)
        return carry

    lax.fori_loop(FIRST, experts, later_maxima, 0)
    pair = send(maxima.at[theirs], partner, pair_send, pair_recv, at((0, 0, 1)))
    pair.start()
    for s in router_y:
        s.wait()
    router_x = [
        send(
            router_ref.at[:, columns(me)],
            router_ref.at[:, columns(me)],
            router_send.at[3 + i],
            router_recv.at[3 + i],
            at(o),
        )
        for i, o in enumerate(SAME_CORE)
    ]
    for s in router_x:
        s.start()
    pair.wait()
    paired[...] = jnp.maximum(maxima[mine], partner[...])
    exchange = [
        send(paired, others.at[i], other_send.at[i], other_recv.at[i], at(o)) for i, o in enumerate(SAME_CORE)
    ]
    for s in exchange:
        s.start()

    top = maxima[0:FIRST]
    for s in straights:
        s.wait()
    for i in range(len(OFFSETS)):
        top = jnp.maximum(top, straight[i])
    scales[0:FIRST] = top

    def parcels(k):
        block = pl.ds(k * STEP, STEP)
        return [
            send(
                narrow.at[block, pl.ds(pl.multiple_of(at(o) * share, share), share), :],
                final_ref.at[block, :, columns(me)],
                send_sem.at[i],
                recv_sem.at[i],
                at(o),
            )
            for i, o in enumerate(OFFSETS)
        ]

    def step(k, carry):
        for e in range(STEP):
            divide(k * STEP + e)

        @pl.when(k > 0)
        def _():
            for s in parcels(k):
                s.wait_send()

        for s in parcels(k):
            s.start()
        for e in range(STEP):
            final_ref[k * STEP + e, :, columns(me)] = narrow[
                k * STEP + e, pl.ds(pl.multiple_of(me * share, share), share), :
            ]
        return carry

    lax.fori_loop(0, FIRST // STEP, step, 0)

    for s in exchange:
        s.wait()
    top = paired[...]
    for i in range(len(SAME_CORE)):
        top = jnp.maximum(top, others[i])
    scales[mine] = top
    back = send(scales.at[mine], scales.at[mine], back_send, back_recv, at((0, 0, 1)))
    back.start()
    back.wait()

    lax.fori_loop(FIRST // STEP, experts // STEP, step, 0)

    for s in router_x:
        s.wait()
    router_core = []
    for i in range(8):
        column = columns(i * 2 + core)
        router_core.append(
            send(router_ref.at[:, column], router_ref.at[:, column], router_send.at[10 + i], router_recv.at[10 + i], at((0, 0, 1)))
        )
    for s in router_core:
        s.start()
    ours = scales[:, pl.ds(me // 2, 1), :].reshape(experts, 128)
    scale_ref[...] = jnp.where(core == 0, ours[:, :share], ours[:, share:])
    for s in router_core:
        s.wait()
    for s in parcels(0):
        s.wait_send()
    for i, o in enumerate(OFFSETS):
        whole = final_ref.at[:, :, columns(at(o, -1))]
        send(whole, whole, send_sem.at[i], recv_sem.at[i], at(o)).wait_recv()


def solution(mesh):
    def shards(master_down, router_weight, router_gain):
        experts, rows, _ = master_down.shape
        half = (experts - FIRST) // 2
        peers, cores = len(OFFSETS), len(SAME_CORE)
        vmem = pl.BlockSpec(memory_space=pltpu.VMEM)
        dma = pltpu.SemaphoreType.DMA
        final_down, scale_down, router = pl.pallas_call(
            functools.partial(kernel, experts, rows),
            out_shape=(
                jax.ShapeDtypeStruct((experts, rows // 16, 2048), jnp.bfloat16),
                jax.ShapeDtypeStruct((experts, rows // 16), jnp.float32),
                jax.ShapeDtypeStruct((64, 2048), jnp.bfloat16),
            ),
            in_specs=[pl.BlockSpec(memory_space=pl.ANY), vmem, vmem],
            out_specs=(vmem, vmem, vmem),
            scratch_shapes=[
                pltpu.VMEM((experts, rows, 128), jnp.float32),
                pltpu.VMEM((experts, rows, 128), jnp.bfloat16),
                pltpu.VMEM((experts, 8, 128), jnp.float32),
                pltpu.VMEM((peers, FIRST, 8, 128), jnp.float32),
                pltpu.VMEM((half, 8, 128), jnp.float32),
                pltpu.VMEM((half, 8, 128), jnp.float32),
                pltpu.VMEM((cores, half, 8, 128), jnp.float32),
                pltpu.VMEM((experts, 8, 128), jnp.float32),
                pltpu.VMEM((16, 128), jnp.bfloat16),
                dma((experts,)),
                dma((peers,)),
                dma((peers,)),
                dma((peers,)),
                dma((peers,)),
                dma,
                dma,
                dma((cores,)),
                dma((cores,)),
                dma,
                dma,
                dma((18,)),
                dma((18,)),
            ],
            compiler_params=pltpu.CompilerParams(
                collective_id=0, has_side_effects=True, vmem_limit_bytes=48 * 2**20
            ),
            name="serve",
        )(master_down, router_weight.T, router_gain[None, :])
        return final_down, scale_down, router.T

    return jax.shard_map(
        shards,
        mesh=mesh,
        in_specs=(
            P(("trial", "ep"), None, "fsdp"),
            P(("trial", "fsdp"), "ep"),
            P(("trial", "fsdp")),
        ),
        out_specs=(P(("trial", "ep"), "fsdp", None), P(("trial", "ep"), "fsdp"), P("trial", None)),
        check_vma=False,
    )
```

time: 195 us -> 124 us (0.64)
  the two profiles are of different devices: /device:TPU:55 before, /device:TPU:1 now
where the time goes in v1:
time: 124 us; the launch traced here: 123 us
  Pallas kernels  118 us (95%)
  local copies, waits for them, and re-layouts  4.66 us (4%)
    pallas_call x1, Pallas kernels, shards(): pl.pallas_call(functools.partial(kernel, experts, rows), out_shape=(jax.S...  118 us
    unnamed x7, local copies, waits for them, and re-layouts  4.66 us

profile of v1, /device:TPU:1, one launch (start us, length us, event | category | flops | bytes accessed | tf_op | source)
XLA Modules:
  0.0 123.4 jit_solution(629252546346222923)
XLA Ops:
  0.6 0.0 copy-start
  0.6 0.7 copy-done
  1.3 0.0 copy-start.1
  1.3 0.7 copy-done.1
  2.0 118.1 %serve.1 = (bf16[16,64,2048]{2,1,0:T(8,128)(2,1)S(1)}, f32[16,64]{1,0:T(8,128)S(1)}, bf16[64,2048]{1,0:T(8,128)(2,1)S(1)}) custom-call(f32[16,1024,128]{2,1,0:T(8,128)} %w_hbm.1, f32[16,128]{1,0:T(8,128)S(1)} %bitcast.4, f32[1,128]{1,0:T(1,128)S(1)} %bitcast.5), custom_call_target="tpu_custom_call" | custom-call | tf_op jit(solution)/shard_map/serve/pallas_call | solution.py:231
  120.1 2.0 %copy.9 = bf16[16,64,2048]{2,1,0:T(8,128)(2,1)} copy(bf16[16,64,2048]{2,1,0:T(8,128)(2,1)S(1)} %get-tuple-element.12) | data formatting | bytes 8388608
  122.1 0.6 copy.10
  122.7 0.7 copy.11
Async XLA Ops:
  0.6 0.7 copy-start
  1.3 0.7 copy-start.1

commit v2 on v1

v2 whole, which is shorter than its diff:
```python
import functools

import jax
import jax.numpy as jnp
from jax import lax
from jax.experimental import pallas as pl
from jax.experimental.pallas import tpu as pltpu
from jax.sharding import PartitionSpec as P

MESH = pl.DeviceIdType.MESH

OFFSETS = [(1, dx, dc) for dx in (0, 1, 3, 2) for dc in (0, 1)] + [
    (0, dx, dc) for dx in (1, 3, 2, 0) for dc in (0, 1) if (dx, dc) != (0, 0)
]
ALONG_X = [(0, dx, 0) for dx in (1, 3, 2)]
ACROSS_Z = (1, 0, 0)
PARTNER = (0, 0, 1)
FIRST = 2
GROUPS = ((2, 8), (8, 16))
RAW = 4
STEP = 2


def kernel(
    experts,
    rows,
    w_hbm,
    rt_hbm,
    gain_hbm,
    final_ref,
    scale_ref,
    router_ref,
    w,
    narrow,
    raw,
    maxima,
    straight,
    partner,
    paired,
    along,
    planed,
    across,
    scales,
    rt,
    gain,
    own_router,
    load_sem,
    send_sem,
    recv_sem,
    raw_send,
    raw_recv,
    straight_send,
    straight_recv,
    pair_send,
    pair_recv,
    along_send,
    along_recv,
    across_send,
    across_recv,
    back_send,
    back_recv,
    router_send,
    router_recv,
):
    trial, ep, me = lax.axis_index("trial"), lax.axis_index("ep"), lax.axis_index("fsdp")
    plane, x, core = me // 8, lax.rem(me // 2, 4), lax.rem(me, 2)
    share = rows // 16
    last = experts - 1

    def at(offset, sign=1):
        dz, dx, dc = offset
        return lax.rem(plane + dz, 2) * 8 + lax.rem(x + 4 + sign * dx, 4) * 2 + lax.rem(core + dc, 2)

    def send(src, dst, send, recv, index, row=None):
        return pltpu.make_async_remote_copy(
            src_ref=src,
            dst_ref=dst,
            send_sem=send,
            recv_sem=recv,
            device_id=(trial, ep if row is None else row, index),
            device_id_type=MESH,
        )

    def columns(index):
        return pl.ds(pl.multiple_of(index * 128, 128), 128)

    def part_of(index):
        return pl.ds(pl.multiple_of(index * share, share), share)

    barrier = pltpu.get_barrier_semaphore()
    for o in OFFSETS:
        pl.semaphore_signal(barrier, inc=1, device_id=(trial, ep, at(o)), device_id_type=MESH)
    for d in (1, 2, 3):
        pl.semaphore_signal(barrier, inc=1, device_id=(trial, lax.rem(ep + d, 4), me), device_id_type=MESH)

    loads = [pltpu.make_async_copy(w_hbm.at[e], w.at[e], load_sem.at[e]) for e in range(experts)]
    rt_load = pltpu.make_async_copy(rt_hbm, rt, load_sem.at[experts])
    gain_load = pltpu.make_async_copy(gain_hbm, gain, load_sem.at[experts + 1])
    for e in range(FIRST):
        loads[e].start()
    rt_load.start()
    gain_load.start()
    loads[last].start()
    for e in range(FIRST, last):
        loads[e].start()

    def take_maxima(e):
        for b in range(rows // 128):
            block = jnp.abs(w[e, b * 128 : (b + 1) * 128, :])
            maxima[e, b : b + 1, :] = jnp.max(block.T, axis=0, keepdims=True)

    def divide(e):
        inverse = 1.0 / scales[e]
        for b in range(rows // 128):
            factor = jnp.broadcast_to(inverse[b : b + 1, :], (128, 128)).T
            narrow[e, b * 128 : (b + 1) * 128, :] = (w[e, b * 128 : (b + 1) * 128, :] * factor).astype(jnp.bfloat16)

    def maxima_of(lo, hi):
        def one(e, carry):
            take_maxima(e)
            return carry

        lax.fori_loop(lo, hi, one, 0)

    with jax.named_scope("first_maxima"):
        for e in range(FIRST):
            loads[e].wait()
        maxima_of(0, FIRST)
    with jax.named_scope("router_part"):
        rt_load.wait()
        gain_load.wait()
        part = (rt[...] * gain[...]).astype(jnp.bfloat16)
        own_router[...] = part
        own_rows = pl.ds(pl.multiple_of(ep * 16, 16), 16)
        router_ref[own_rows, columns(me)] = part
    with jax.named_scope("maxima_a"):
        for e in range(FIRST, experts):
            loads[e].wait()
        maxima_of(*GROUPS[0])
    with jax.named_scope("barrier_wait"):
        pl.semaphore_wait(barrier, len(OFFSETS) + 3)

    straights = [
        send(maxima.at[pl.ds(0, FIRST)], straight.at[i], straight_send.at[i], straight_recv.at[i], at(o))
        for i, o in enumerate(OFFSETS)
    ]
    for s in straights:
        s.start()

    halves, kept, taken = [], [], 0
    for lo, hi in GROUPS:
        half = (hi - lo) // 2
        halves.append((pl.ds(lo + core * half, half), pl.ds(lo + (1 - core) * half, half)))
        kept.append(pl.ds(taken, half))
        taken += half
    pairs = [
        send(maxima.at[theirs], partner.at[k], pair_send.at[g], pair_recv.at[g], at(PARTNER))
        for g, ((_, theirs), k) in enumerate(zip(halves, kept))
    ]
    alongs = [
        [
            send(paired.at[k], along.at[i, k], along_send.at[g, i], along_recv.at[g, i], at(o))
            for i, o in enumerate(ALONG_X)
        ]
        for g, k in enumerate(kept)
    ]
    acrosses = [
        send(planed.at[k], across.at[k], across_send.at[g], across_recv.at[g], at(ACROSS_Z))
        for g, k in enumerate(kept)
    ]
    backs = [
        send(scales.at[mine], scales.at[mine], back_send.at[g], back_recv.at[g], at(PARTNER))
        for g, (mine, _) in enumerate(halves)
    ]
    raws = [
        send(w.at[last, part_of(at(o)), :], raw.at[i], raw_send.at[i], raw_recv.at[i], at(o))
        for i, o in enumerate(OFFSETS[:RAW])
    ]

    pairs[0].start()
    for s in raws:
        s.start()
    router_y = [
        send(own_router, router_ref.at[own_rows, columns(me)], router_send.at[d - 1], router_recv.at[d - 1], me, lax.rem(ep + d, 4))
        for d in (1, 2, 3)
    ]
    for s in router_y:
        s.start()

    def reduce_pair(g):
        pairs[g].wait()
        paired[kept[g]] = jnp.maximum(maxima[halves[g][0]], partner[kept[g]])
        for s in alongs[g]:
            s.start()

    def reduce_along(g):
        for s in alongs[g]:
            s.wait()
        top = paired[kept[g]]
        for i in range(len(ALONG_X)):
            top = jnp.maximum(top, along[i, kept[g]])
        planed[kept[g]] = top
        acrosses[g].start()

    def reduce_across(g):
        acrosses[g].wait()
        scales[halves[g][0]] = jnp.maximum(planed[kept[g]], across[kept[g]])
        backs[g].start()

    with jax.named_scope("pair_a"):
        reduce_pair(0)
    with jax.named_scope("maxima_b"):
        maxima_of(*GROUPS[1])
        pairs[1].start()
    with jax.named_scope("router_y"):
        for s in router_y:
            s.wait()
    router_x = [
        send(router_ref.at[:, columns(me)], router_ref.at[:, columns(me)], router_send.at[3 + i], router_recv.at[3 + i], at(o))
        for i, o in enumerate(ALONG_X + [ACROSS_Z])
    ]
    for s in router_x:
        s.start()
    with jax.named_scope("pair_b"):
        reduce_pair(1)
    with jax.named_scope("along_a"):
        reduce_along(0)
    with jax.named_scope("along_b"):
        reduce_along(1)

    with jax.named_scope("straight_wait"):
        for s in straights:
            s.wait()
        top = maxima[0:FIRST]
        for i in range(len(OFFSETS)):
            top = jnp.maximum(top, straight[i])
        scales[0:FIRST] = top

    def parcel(block, i, slot):
        o = OFFSETS[i]
        return send(
            narrow.at[block, part_of(at(o)), :],
            final_ref.at[block, :, columns(me)],
            send_sem.at[slot, i],
            recv_sem.at[i],
            at(o),
        )

    peers = range(len(OFFSETS))

    def keep(e):
        final_ref[e, :, columns(me)] = narrow[e, part_of(me), :]

    def step(k, carry):
        block = pl.ds(k * STEP, STEP)
        slot = lax.rem(k, 2)
        with jax.named_scope("divide"):
            for e in range(STEP):
                divide(k * STEP + e)

        with jax.named_scope("send_wait"):
            @pl.when(k > 1)
            def _():
                for i in peers:
                    parcel(block, i, slot).wait_send()

        for i in peers:
            parcel(block, i, slot).start()
        for e in range(STEP):
            keep(k * STEP + e)
        return carry

    lax.fori_loop(0, FIRST // STEP, step, 0)
    for g in range(len(GROUPS)):
        with jax.named_scope(f"across_{g}"):
            reduce_across(g)
    for g in range(len(GROUPS)):
        with jax.named_scope(f"back_{g}"):
            backs[g].wait()
    steps = experts // STEP
    lax.fori_loop(FIRST // STEP, steps - 1, step, 0)

    for e in range(STEP):
        divide(experts - STEP + e)
    end = (steps - 1) % 2
    for i in peers:
        parcel(pl.ds(0, STEP), i, end).wait_send()
    ends = [parcel(pl.ds(experts - STEP, STEP - 1 if i < RAW else STEP), i, end) for i in peers]
    for s in ends:
        s.start()
    for e in range(STEP):
        keep(experts - STEP + e)

    ours = scales[:, pl.ds(me // 2, 1), :].reshape(experts, 128)
    scale_ref[...] = jnp.where(core == 0, ours[:, :share], ours[:, share:])
    factor = jnp.broadcast_to(1.0 / ours[last:], (128, 128)).T
    factor = jnp.where(core == 0, factor[:share], factor[share:])
    for i in range(RAW):
        raws[i].wait()
        final_ref[last, :, columns(at(OFFSETS[i], -1))] = (raw[i] * factor).astype(jnp.bfloat16)

    with jax.named_scope("router_x"):
        for s in router_x:
            s.wait()
    sides = [at(o) for o in ALONG_X] + [me]
    across_z = lax.rem(me + 8, 16)
    router_far = [
        send(router_ref.at[:, columns(across_z)], router_ref.at[:, columns(across_z)], router_send.at[7 + i], router_recv.at[7 + i], at(o))
        for i, o in enumerate(ALONG_X)
    ]
    for s in router_far:
        s.start()
    for s in router_far:
        s.wait()
    router_core = []
    for i in range(8):
        column = columns(i * 2 + core)
        router_core.append(
            send(router_ref.at[:, column], router_ref.at[:, column], router_send.at[10 + i], router_recv.at[10 + i], at(PARTNER))
        )
    for s in router_core:
        s.start()
    for s in router_core:
        s.wait()
    with jax.named_scope("last_waits"):
        for i in peers:
            parcel(pl.ds(0, STEP), i, 1 - end).wait_send()
            ends[i].wait_send()
        for i, o in enumerate(OFFSETS):
            whole = final_ref.at[pl.ds(0, last if i < RAW else experts), :, columns(at(o, -1))]
            send(whole, whole, send_sem.at[0, i], recv_sem.at[i], at(o)).wait_recv()


def place(final_in, scale_in, router_in, final_out, scale_out, router_out, sem):
    copies = [
        pltpu.make_async_copy(src, dst, sem.at[i])
        for i, (src, dst) in enumerate(((final_in, final_out), (scale_in, scale_out), (router_in, router_out)))
    ]
    for c in copies:
        c.start()
    for c in copies:
        c.wait()


def solution(mesh):
    def shards(master_down, router_weight, router_gain):
        experts, rows, _ = master_down.shape
        held = sum(hi - lo for lo, hi in GROUPS) // 2
        peers, groups, sides = len(OFFSETS), len(GROUPS), len(ALONG_X)
        vmem = pl.BlockSpec(memory_space=pltpu.VMEM)
        hbm = pl.BlockSpec(memory_space=pltpu.HBM)
        dma = pltpu.SemaphoreType.DMA
        shapes = (
            jax.ShapeDtypeStruct((experts, rows // 16, 2048), jnp.bfloat16),
            jax.ShapeDtypeStruct((experts, rows // 16), jnp.float32),
            jax.ShapeDtypeStruct((64, 2048), jnp.bfloat16),
        )
        tile = (8, 128)
        results = pl.pallas_call(
            functools.partial(kernel, experts, rows),
            out_shape=shapes,
            in_specs=[hbm] * 3,
            out_specs=(vmem, vmem, vmem),
            scratch_shapes=[
                pltpu.VMEM((experts, rows, 128), jnp.float32),
                pltpu.VMEM((experts, rows, 128), jnp.bfloat16),
                pltpu.VMEM((RAW, rows // 16, 128), jnp.float32),
                pltpu.VMEM((experts, *tile), jnp.float32),
                pltpu.VMEM((peers, FIRST, *tile), jnp.float32),
                pltpu.VMEM((held, *tile), jnp.float32),
                pltpu.VMEM((held, *tile), jnp.float32),
                pltpu.VMEM((sides, held, *tile), jnp.float32),
                pltpu.VMEM((held, *tile), jnp.float32),
                pltpu.VMEM((held, *tile), jnp.float32),
                pltpu.VMEM((experts, *tile), jnp.float32),
                pltpu.VMEM((16, 128), jnp.float32),
                pltpu.VMEM((1, 128), jnp.float32),
                pltpu.VMEM((16, 128), jnp.bfloat16),
                dma((experts + 2,)),
                dma((2, peers)),
                dma((peers,)),
                dma((RAW,)),
                dma((RAW,)),
                dma((peers,)),
                dma((peers,)),
                dma((groups,)),
                dma((groups,)),
                dma((groups, sides)),
                dma((groups, sides)),
                dma((groups,)),
                dma((groups,)),
                dma((groups,)),
                dma((groups,)),
                dma((18,)),
                dma((18,)),
            ],
            compiler_params=pltpu.CompilerParams(
                collective_id=0, has_side_effects=True, vmem_limit_bytes=48 * 2**20
            ),
            name="serve",
        )(master_down, *(pltpu.with_memory_space_constraint(a, pltpu.HBM) for a in (router_weight.T, router_gain[None, :])))
        final_down, scale_down, router = pl.pallas_call(
            place,
            out_shape=shapes,
            in_specs=[pl.BlockSpec(memory_space=pl.ANY)] * 3,
            out_specs=(hbm,) * 3,
            scratch_shapes=[dma((3,))],
            compiler_params=pltpu.CompilerParams(vmem_limit_bytes=8 * 2**20),
            name="place",
        )(*results)
        return final_down, scale_down, router.T

    return jax.shard_map(
        shards,
        mesh=mesh,
        in_specs=(
            P(("trial", "ep"), None, "fsdp"),
            P(("trial", "fsdp"), "ep"),
            P(("trial", "fsdp")),
        ),
        out_specs=(P(("trial", "ep"), "fsdp", None), P(("trial", "ep"), "fsdp"), P("trial", None)),
        check_vma=False,
    )
```

time: 124 us -> 118 us (0.952)
  local copies, waits for them, and re-layouts: 4.66 us -> 0 us
    unnamed x7 -> x0, local copies, waits for them, and re-layouts: 4.66 us -> none
    pallas_call x1 -> x2, Pallas kernels: 118 us -> 118 us  [the longest x1 116 us: shards(): pl.pallas_call(functools.partial(kernel, experts, rows), out_shape=shapes...]
where the time goes in v2:
time: 118 us
  Pallas kernels  118 us (100%)
    pallas_call x1, Pallas kernels, shards(): pl.pallas_call(functools.partial(kernel, experts, rows), out_shape=shapes...  116 us

profile of v2, /device:TPU:1, one launch (start us, length us, event | category | flops | bytes accessed | tf_op | source)
XLA Modules:
  0.0 118.3 jit_solution(9934313767617699035)
XLA Ops:
  0.6 115.5 %serve.1 = (bf16[16,64,2048]{2,1,0:T(8,128)(2,1)S(1)}, f32[16,64]{1,0:T(8,128)S(1)}, bf16[64,2048]{1,0:T(8,128)(2,1)S(1)}) custom-call(f32[16,1024,128]{2,1,0:T(8,128)} %w_hbm.1, f32[16,128]{1,0:T(8,128)} %bitcast.3, f32[1,128]{1,0:T(1,128)} %bitcast.4), custom_call_target="tpu_custom_call" | custom-call | tf_op jit(solution)/shard_map/serve/pallas_call | solution.py:359
  116.2 2.1 %place.1 = (bf16[16,64,2048]{2,1,0:T(8,128)(2,1)}, f32[16,64]{1,0:T(8,128)}, bf16[64,2048]{1,0:T(8,128)(2,1)}) custom-call(bf16[16,64,2048]{2,1,0:T(8,128)(2,1)S(1)} %get-tuple-element.9.final_in, f32[16,64]{1,0:T(8,128)S(1)} %get-tuple-element.10.scale_in, bf16[64,2048]{1,0:T(8,128)(2,1)S(1)} %get-tuple-element.11.router_in), custom_call_target="tpu_custom_call" | custom-call | tf_op jit(solution)/shard_map/place/pallas_call | solution.py:402

commit v3 on v2

v3 whole, which is shorter than its diff:
```python
import functools

import jax
import jax.numpy as jnp
from jax import lax
from jax.experimental import pallas as pl
from jax.experimental.pallas import tpu as pltpu
from jax.sharding import PartitionSpec as P

MESH = pl.DeviceIdType.MESH

OFFSETS = [(1, dx, dc) for dx in (0, 1, 3, 2) for dc in (0, 1)] + [
    (0, dx, dc) for dx in (1, 3, 2, 0) for dc in (0, 1) if (dx, dc) != (0, 0)
]
ALONG_X = [(0, dx, 0) for dx in (1, 3, 2)]
ACROSS_Z = (1, 0, 0)
PARTNER = (0, 0, 1)
ACROSS = OFFSETS[:8]
FIRST = 3
RAW = (2, 4)
WINDOW = 4
LEFT = 2


def kernel(
    experts,
    rows,
    w_hbm,
    rt_hbm,
    gain_hbm,
    final_ref,
    scale_ref,
    router_ref,
    w,
    narrow,
    raw,
    maxima,
    straight,
    early,
    partner,
    paired,
    along,
    planed,
    across,
    scales,
    rt,
    gain,
    own_router,
    load_sem,
    send_sem,
    recv_sem,
    raw_send,
    raw_recv,
    straight_send,
    straight_recv,
    pair_send,
    pair_recv,
    along_send,
    along_recv,
    across_send,
    across_recv,
    back_send,
    back_recv,
    router_send,
    router_recv,
    go,
    gate,
):
    trial, ep, me = lax.axis_index("trial"), lax.axis_index("ep"), lax.axis_index("fsdp")
    z_first = trial < 2
    plane, x, core = me // 8, lax.rem(me // 2, 4), lax.rem(me, 2)
    share = rows // 16
    last = experts - 1

    def at(offset, sign=1):
        dz, dx, dc = offset
        return lax.rem(plane + dz, 2) * 8 + lax.rem(x + 4 + sign * dx, 4) * 2 + lax.rem(core + dc, 2)

    def send(src, dst, send, recv, index, row=None):
        return pltpu.make_async_remote_copy(
            src_ref=src,
            dst_ref=dst,
            send_sem=send,
            recv_sem=recv,
            device_id=(trial, ep if row is None else row, index),
            device_id_type=MESH,
        )

    def columns(index):
        return pl.ds(pl.multiple_of(index * 128, 128), 128)

    def part_of(index):
        return pl.ds(pl.multiple_of(index * share, share), share)

    barrier = pltpu.get_barrier_semaphore()
    for o in OFFSETS:
        pl.semaphore_signal(barrier, inc=1, device_id=(trial, ep, at(o)), device_id_type=MESH)
    for d in (1, 2, 3):
        pl.semaphore_signal(barrier, inc=1, device_id=(trial, lax.rem(ep + d, 4), me), device_id_type=MESH)
    sharers = [(lax.rem(trial + 2, 4), ep, at(o)) for o in ((0, 0, 0), ACROSS_Z)]
    gated = lax.rem(me + 8 * lax.rem(trial, 2), 16)
    for d in sharers:
        pl.semaphore_signal(barrier, inc=1, device_id=d, device_id_type=MESH)

    loads = [pltpu.make_async_copy(w_hbm.at[e], w.at[e], load_sem.at[e]) for e in range(experts)]
    rt_load = pltpu.make_async_copy(rt_hbm, rt, load_sem.at[experts])
    gain_load = pltpu.make_async_copy(gain_hbm, gain, load_sem.at[experts + 1])
    for e in range(FIRST):
        loads[e].start()
    rt_load.start()
    gain_load.start()
    loads[last].start()
    for e in range(FIRST, last):
        loads[e].start()

    def take_maxima(e):
        for b in range(rows // 128):
            block = jnp.abs(w[e, b * 128 : (b + 1) * 128, :])
            maxima[e, b : b + 1, :] = jnp.max(block.T, axis=0, keepdims=True)

    def divide(e, scale):
        inverse = 1.0 / scale
        for b in range(rows // 128):
            factor = jnp.broadcast_to(inverse[b : b + 1, :], (128, 128)).T
            narrow[e, b * 128 : (b + 1) * 128, :] = (w[e, b * 128 : (b + 1) * 128, :] * factor).astype(jnp.bfloat16)

    def maxima_of(lo, hi):
        def one(e, carry):
            pltpu.make_async_copy(w_hbm.at[e], w.at[e], load_sem.at[e]).wait()
            take_maxima(e)
            return carry

        lax.fori_loop(lo, hi, one, 0)

    with jax.named_scope("first_maxima"):
        maxima_of(0, FIRST)
    with jax.named_scope("router_part"):
        rt_load.wait()
        gain_load.wait()
        part = (rt[...] * gain[...]).astype(jnp.bfloat16)
        own_router[...] = part
        own_rows = pl.ds(pl.multiple_of(ep * 16, 16), 16)
        router_ref[own_rows, columns(me)] = part
    loads[last].wait()

    def other_maxima():
        with jax.named_scope("other_maxima"):
            maxima_of(FIRST, last)
            take_maxima(last)

    straights = [
        send(maxima.at[pl.ds(0, FIRST)], straight.at[i], straight_send, straight_recv, at(o))
        for i, o in enumerate(OFFSETS)
    ]
    raws = [
        send(w.at[last, part_of(at(o)), :], raw.at[i], raw_send, raw_recv, at(o))
        for i, o in enumerate(ACROSS)
    ]
    router_y = [
        send(own_router, router_ref.at[own_rows, columns(me)], router_send.at[0], router_recv.at[0], me, lax.rem(ep + d, 4))
        for d in (1, 2, 3)
    ]
    router_z = send(own_router, router_ref.at[own_rows, columns(me)], router_send.at[1], router_recv.at[1], at(ACROSS_Z))
    half = experts // 2
    mine, theirs = pl.ds(core * half, half), pl.ds((1 - core) * half, half)
    pair = send(maxima.at[theirs], partner, pair_send, pair_recv, at(PARTNER))
    along_x = [send(planed, along.at[i], along_send, along_recv, at(o)) for i, o in enumerate(ALONG_X)]
    across_z = send(paired, across, across_send, across_recv, at(ACROSS_Z))
    back = send(scales.at[mine], scales.at[mine], back_send, back_recv, at(PARTNER))

    @pl.when(jnp.logical_not(z_first))
    def _():
        other_maxima()

    with jax.named_scope("barrier_wait"):
        pl.semaphore_wait(barrier, len(OFFSETS) + 3 + len(sharers))

    @pl.when(z_first)
    def _():
        for s in straights + raws[: RAW[0]] + router_y + [router_z]:
            s.start()
        other_maxima()
        pair.start()

    @pl.when(jnp.logical_not(z_first))
    def _():
        for s in [pair] + router_y + [router_z]:
            s.start()

    with jax.named_scope("pair"):
        pair.wait()
        paired[...] = jnp.maximum(maxima[mine], partner[...])
    across_z.start()

    @pl.when(jnp.logical_not(z_first))
    def _():
        with jax.named_scope("gate_open"):
            across_z.wait_send()
            router_z.wait_send()
            pl.semaphore_signal(gate, inc=1, device_id=(lax.rem(trial + 2, 4), ep, gated), device_id_type=MESH)
            for s in raws[: RAW[1]]:
                s.start()

    everyone = list(enumerate(OFFSETS))
    far, near = everyone[:8], everyone[8:]

    def parcel(e, i, o):
        block = pl.ds(e, 1)
        return send(
            narrow.at[block, part_of(at(o)), :],
            final_ref.at[block, :, columns(me)],
            send_sem.at[lax.rem(e, WINDOW), i // 8],
            recv_sem.at[i],
            at(o),
        )

    def await_sent(e, which):
        if which:
            size = narrow.at[0, pl.ds(0, share * len(which)), :]
            send(size, size, send_sem.at[lax.rem(e, WINDOW), which[0][0] // 8], recv_sem.at[0], me).wait_send()

    def step(e, which):
        with jax.named_scope("send_wait"):
            if not isinstance(e, int):
                @pl.when(e >= WINDOW)
                def _():
                    await_sent(e, which)

        for i, o in which:
            parcel(e, i, o).start()

    def fresh(e, scale):
        with jax.named_scope("divide"):
            divide(e, scale)
        final_ref[e, :, columns(me)] = narrow[e, part_of(me), :]

    def steps(lo, hi, which, first):
        def one(e, carry):
            if first:
                fresh(e, scales[e])
            step(e, which)
            return carry

        lax.fori_loop(lo, hi, one, 0)

    @pl.when(z_first)
    def _():
        with jax.named_scope("straight_wait"):
            send(straight, straight, straight_send, straight_recv, me).wait()
            top = maxima[0:FIRST]
            for i in range(len(OFFSETS)):
                top = jnp.maximum(top, straight[i])
            early[...] = top
        for e in range(FIRST):
            fresh(e, early[e])
        with jax.named_scope("gate_wait"):
            pl.semaphore_wait(gate, 1)
        for e in range(FIRST):
            step(e, far)
        across_z.wait_send()

    with jax.named_scope("across"):
        across_z.wait_recv()
        planed[...] = jnp.maximum(paired[...], across[...])
    for s in along_x:
        s.start()
    with jax.named_scope("along"):
        send(along, along, along_send, along_recv, me).wait()
        top = planed[...]
        for i in range(len(ALONG_X)):
            top = jnp.maximum(top, along[i])
        scales[mine] = top
    back.start()
    with jax.named_scope("back"):
        back.wait()

    ours = scales[:, pl.ds(me // 2, 1), :].reshape(experts, 128)
    scale_ref[...] = jnp.where(core == 0, ours[:, :share], ours[:, share:])

    opposite = lax.rem(me + 8, 16)
    theirs_y = router_ref.at[own_rows, columns(opposite)]
    router_y2 = [
        send(theirs_y, theirs_y, router_send.at[2], router_recv.at[2], me, lax.rem(ep + d, 4)) for d in (1, 2, 3)
    ]
    router_x = [
        send(router_ref.at[:, columns(c)], router_ref.at[:, columns(c)], router_send.at[3], router_recv.at[3], at(o))
        for c in (me, opposite)
        for o in ALONG_X
    ]
    router_core = [
        send(router_ref.at[:, columns(c)], router_ref.at[:, columns(c)], router_send.at[4], router_recv.at[4], at(PARTNER))
        for c in [i * 2 + core for i in range(8)]
    ]

    def finish_router():
        with jax.named_scope("router_rest"):
            def arrived(which, blocks, columns_of):
                size = router_ref.at[pl.ds(0, 16 * blocks), pl.ds(0, 128 * columns_of)]
                send(size, size, router_send.at[which], router_recv.at[which], me).wait()

            arrived(0, 3, 1)
            router_z.wait_recv()
            for s in router_y2:
                s.start()
            arrived(2, 3, 1)
            for s in router_x:
                s.start()
            arrived(3, 4, 6)
            for s in router_core:
                s.start()
            arrived(4, 4, 8)

    def take_raw(count):
        with jax.named_scope("raw"):
            factor = jnp.broadcast_to(1.0 / ours[last:], (128, 128)).T
            factor = jnp.where(core == 0, factor[:share], factor[share:])
            if count:
                size = raw.at[pl.ds(0, count)]
                send(size, size, raw_send, raw_recv, me).wait()
            for i, o in enumerate(ACROSS[:count]):
                final_ref[last, :, columns(at(o, -1))] = (raw[i] * factor).astype(jnp.bfloat16)

    def received(which, count):
        for i, o in which:
            whole = final_ref.at[pl.ds(0, count), :, columns(at(o, -1))]
            send(whole, whole, send_sem.at[0, 0], recv_sem.at[i], at(o)).wait_recv()

    @pl.when(z_first)
    def _():
        with jax.named_scope("far_first"):
            steps(FIRST, last, far, True)
            fresh(last, scales[last])
            await_sent(last - WINDOW, far)
            for i, o in far[RAW[0] :]:
                parcel(last, i, o).start()
        with jax.named_scope("far_sent"):
            router_z.wait_send()
            for e in range(last - WINDOW + 1, last - LEFT + 1):
                await_sent(e, far)
            for d in sharers:
                pl.semaphore_signal(go, inc=1, device_id=d, device_id_type=MESH)
        take_raw(RAW[0])
        finish_router()
        with jax.named_scope("near_second"):
            steps(0, experts, near, False)
        with jax.named_scope("last_sends"):
            for e in range(last - LEFT + 1, last):
                await_sent(e, far)
            await_sent(last, far[RAW[0] :])
            for e in range(experts - WINDOW, experts):
                await_sent(e, near)
        with jax.named_scope("last_far"):
            received(far[: RAW[0]], last)
            received(far[RAW[0] :], experts)

    @pl.when(jnp.logical_not(z_first))
    def _():
        with jax.named_scope("near_first"):
            steps(0, experts, near, True)
        finish_router()
        with jax.named_scope("go_wait"):
            pl.semaphore_wait(go, len(sharers))
        with jax.named_scope("far_second"):
            steps(0, last, far, False)
            await_sent(last - WINDOW, far)
            for i, o in far[RAW[1] :]:
                parcel(last, i, o).start()
        take_raw(RAW[1])
        with jax.named_scope("last_sends"):
            for e in range(experts - WINDOW, experts):
                await_sent(e, near)
            for e in range(last - WINDOW + 1, last):
                await_sent(e, far)
            await_sent(last, far[RAW[1] :])
        with jax.named_scope("last_far"):
            received(far[: RAW[1]], last)
            received(far[RAW[1] :], experts)

    with jax.named_scope("last_near"):
        received(near, experts)


def place(final_in, scale_in, router_in, final_out, scale_out, router_out, sem):
    copies = [
        pltpu.make_async_copy(src, dst, sem.at[i])
        for i, (src, dst) in enumerate(((final_in, final_out), (scale_in, scale_out), (router_in, router_out)))
    ]
    for c in copies:
        c.start()
    for c in copies:
        c.wait()


def solution(mesh):
    def shards(master_down, router_weight, router_gain):
        experts, rows, _ = master_down.shape
        held = experts // 2
        peers, sides = len(OFFSETS), len(ALONG_X)
        vmem = pl.BlockSpec(memory_space=pltpu.VMEM)
        hbm = pl.BlockSpec(memory_space=pltpu.HBM)
        dma = pltpu.SemaphoreType.DMA
        shapes = (
            jax.ShapeDtypeStruct((experts, rows // 16, 2048), jnp.bfloat16),
            jax.ShapeDtypeStruct((experts, rows // 16), jnp.float32),
            jax.ShapeDtypeStruct((64, 2048), jnp.bfloat16),
        )
        tile = (8, 128)
        results = pl.pallas_call(
            functools.partial(kernel, experts, rows),
            out_shape=shapes,
            in_specs=[hbm] * 3,
            out_specs=(vmem, vmem, vmem),
            scratch_shapes=[
                pltpu.VMEM((experts, rows, 128), jnp.float32),
                pltpu.VMEM((experts, rows, 128), jnp.bfloat16),
                pltpu.VMEM((len(ACROSS), rows // 16, 128), jnp.float32),
                pltpu.VMEM((experts, *tile), jnp.float32),
                pltpu.VMEM((peers, FIRST, *tile), jnp.float32),
                pltpu.VMEM((FIRST, *tile), jnp.float32),
                pltpu.VMEM((held, *tile), jnp.float32),
                pltpu.VMEM((held, *tile), jnp.float32),
                pltpu.VMEM((sides, held, *tile), jnp.float32),
                pltpu.VMEM((held, *tile), jnp.float32),
                pltpu.VMEM((held, *tile), jnp.float32),
                pltpu.VMEM((experts, *tile), jnp.float32),
                pltpu.VMEM((16, 128), jnp.float32),
                pltpu.VMEM((1, 128), jnp.float32),
                pltpu.VMEM((16, 128), jnp.bfloat16),
                dma((experts + 2,)),
                dma((WINDOW, 2)),
                dma((peers,)),
                *[dma] * 12,
                dma((5,)),
                dma((5,)),
                pltpu.SemaphoreType.REGULAR,
                pltpu.SemaphoreType.REGULAR,
            ],
            compiler_params=pltpu.CompilerParams(
                collective_id=0, has_side_effects=True, vmem_limit_bytes=48 * 2**20
            ),
            name="serve",
        )(master_down, *(pltpu.with_memory_space_constraint(a, pltpu.HBM) for a in (router_weight.T, router_gain[None, :])))
        final_down, scale_down, router = pl.pallas_call(
            place,
            out_shape=shapes,
            in_specs=[pl.BlockSpec(memory_space=pl.ANY)] * 3,
            out_specs=(hbm,) * 3,
            scratch_shapes=[dma((3,))],
            compiler_params=pltpu.CompilerParams(vmem_limit_bytes=8 * 2**20),
            name="place",
        )(*results)
        return final_down, scale_down, router.T

    return jax.shard_map(
        shards,
        mesh=mesh,
        in_specs=(
            P(("trial", "ep"), None, "fsdp"),
            P(("trial", "fsdp"), "ep"),
            P(("trial", "fsdp")),
        ),
        out_specs=(P(("trial", "ep"), "fsdp", None), P(("trial", "ep"), "fsdp"), P("trial", None)),
        check_vma=False,
    )
```

time: 118 us -> 115 us (0.975)
  the two profiles are of different devices: /device:TPU:1 before, /device:TPU:65 now
where the time goes in v3:
time: 115 us
  Pallas kernels  115 us (100%)
    pallas_call x1, Pallas kernels, shards(): pl.pallas_call(functools.partial(kernel, experts, rows), out_shape=shapes...  113 us

profile of v3, /device:TPU:65, one launch (start us, length us, event | category | flops | bytes accessed | tf_op | source)
XLA Modules:
  0.0 115.4 jit_solution(3565662929127370501)
XLA Ops:
  0.6 112.6 %serve.1 = (bf16[16,64,2048]{2,1,0:T(8,128)(2,1)S(1)}, f32[16,64]{1,0:T(8,128)S(1)}, bf16[64,2048]{1,0:T(8,128)(2,1)S(1)}) custom-call(f32[16,1024,128]{2,1,0:T(8,128)} %w_hbm.1, f32[16,128]{1,0:T(8,128)} %bitcast.3, f32[1,128]{1,0:T(1,128)} %bitcast.4), custom_call_target="tpu_custom_call" | custom-call | tf_op jit(solution)/shard_map/serve/pallas_call | solution.py:408
  113.3 2.1 %place.1 = (bf16[16,64,2048]{2,1,0:T(8,128)(2,1)}, f32[16,64]{1,0:T(8,128)}, bf16[64,2048]{1,0:T(8,128)(2,1)}) custom-call(bf16[16,64,2048]{2,1,0:T(8,128)(2,1)S(1)} %get-tuple-element.9.final_in, f32[16,64]{1,0:T(8,128)S(1)} %get-tuple-element.10.scale_in, bf16[64,2048]{1,0:T(8,128)(2,1)S(1)} %get-tuple-element.11.router_in), custom_call_target="tpu_custom_call" | custom-call | tf_op jit(solution)/shard_map/place/pallas_call | solution.py:443

commit v4 on v3

--- a/solution.py
+++ b/solution.py
@@ -9,7 +9,7 @@
 
 MESH = pl.DeviceIdType.MESH
 
-OFFSETS = [(1, dx, dc) for dx in (0, 1, 3, 2) for dc in (0, 1)] + [
+OFFSETS = [(1, dx, dc) for dx in (2, 1, 3, 0) for dc in (0, 1)] + [
     (0, dx, dc) for dx in (1, 3, 2, 0) for dc in (0, 1) if (dx, dc) != (0, 0)
 ]
 ALONG_X = [(0, dx, 0) for dx in (1, 3, 2)]
@@ -17,7 +17,7 @@
 PARTNER = (0, 0, 1)
 ACROSS = OFFSETS[:8]
 FIRST = 3
-RAW = (2, 4)
+RAW = (2, 1)
 WINDOW = 4
 LEFT = 2
 
@@ -251,11 +251,12 @@
             for i in range(len(OFFSETS)):
                 top = jnp.maximum(top, straight[i])
             early[...] = top
-        for e in range(FIRST):
-            fresh(e, early[e])
+        fresh(0, early[0])
         with jax.named_scope("gate_wait"):
             pl.semaphore_wait(gate, 1)
-        for e in range(FIRST):
+        step(0, far)
+        for e in range(1, FIRST):
+            fresh(e, early[e])
             step(e, far)
         across_z.wait_send()
 

time: 115 us -> 113 us (0.983)
  Pallas kernels: 115 us -> 112 us
    pallas_call x1, Pallas kernels: 113 us -> 110 us  [shards(): pl.pallas_call(functools.partial(kernel, experts, rows), out_shape=shapes...]
where the time goes in v4:
time: 113 us
  Pallas kernels  112 us (99%)
    pallas_call x1, Pallas kernels, shards(): pl.pallas_call(functools.partial(kernel, experts, rows), out_shape=shapes...  110 us

profile of v4, /device:TPU:65, one launch (start us, length us, event | category | flops | bytes accessed | tf_op | source)
XLA Modules:
  0.0 112.9 jit_solution(5868870656823011225)
XLA Ops:
  0.6 110.2 %serve.1 = (bf16[16,64,2048]{2,1,0:T(8,128)(2,1)S(1)}, f32[16,64]{1,0:T(8,128)S(1)}, bf16[64,2048]{1,0:T(8,128)(2,1)S(1)}) custom-call(f32[16,1024,128]{2,1,0:T(8,128)} %w_hbm.1, f32[16,128]{1,0:T(8,128)} %bitcast.3, f32[1,128]{1,0:T(1,128)} %bitcast.4), custom_call_target="tpu_custom_call" | custom-call | tf_op jit(solution)/shard_map/serve/pallas_call | solution.py:409
  110.8 2.1 %place.1 = (bf16[16,64,2048]{2,1,0:T(8,128)(2,1)}, f32[16,64]{1,0:T(8,128)}, bf16[64,2048]{1,0:T(8,128)(2,1)}) custom-call(bf16[16,64,2048]{2,1,0:T(8,128)(2,1)S(1)} %get-tuple-element.9.final_in, f32[16,64]{1,0:T(8,128)S(1)} %get-tuple-element.10.scale_in, bf16[64,2048]{1,0:T(8,128)(2,1)S(1)} %get-tuple-element.11.router_in), custom_call_target="tpu_custom_call" | custom-call | tf_op jit(solution)/shard_map/place/pallas_call | solution.py:444

commit v5 on v4

--- a/solution.py
+++ b/solution.py
@@ -149,7 +149,8 @@
             take_maxima(last)
 
     straights = [
-        send(maxima.at[pl.ds(0, FIRST)], straight.at[i], straight_send, straight_recv, at(o))
+        send(maxima.at[e], straight.at[e, i], straight_send.at[e], straight_recv.at[e], at(o))
+        for e in range(FIRST)
         for i, o in enumerate(OFFSETS)
     ]
     raws = [
@@ -245,18 +246,17 @@
 
     @pl.when(z_first)
     def _():
-        with jax.named_scope("straight_wait"):
-            send(straight, straight, straight_send, straight_recv, me).wait()
-            top = maxima[0:FIRST]
+        for e in range(FIRST):
+            with jax.named_scope("straight_wait"):
+                send(straight.at[e], straight.at[e], straight_send.at[e], straight_recv.at[e], me).wait()
+            top = maxima[e]
             for i in range(len(OFFSETS)):
-                top = jnp.maximum(top, straight[i])
-            early[...] = top
-        fresh(0, early[0])
-        with jax.named_scope("gate_wait"):
-            pl.semaphore_wait(gate, 1)
-        step(0, far)
-        for e in range(1, FIRST):
+                top = jnp.maximum(top, straight[e, i])
+            early[e] = top
             fresh(e, early[e])
+            if e == 0:
+                with jax.named_scope("gate_wait"):
+                    pl.semaphore_wait(gate, 1)
             step(e, far)
         across_z.wait_send()
 
@@ -416,7 +416,7 @@
                 pltpu.VMEM((experts, rows, 128), jnp.bfloat16),
                 pltpu.VMEM((len(ACROSS), rows // 16, 128), jnp.float32),
                 pltpu.VMEM((experts, *tile), jnp.float32),
-                pltpu.VMEM((peers, FIRST, *tile), jnp.float32),
+                pltpu.VMEM((FIRST, peers, *tile), jnp.float32),
                 pltpu.VMEM((FIRST, *tile), jnp.float32),
                 pltpu.VMEM((held, *tile), jnp.float32),
                 pltpu.VMEM((held, *tile), jnp.float32),
@@ -430,7 +430,11 @@
                 dma((experts + 2,)),
                 dma((WINDOW, 2)),
                 dma((peers,)),
-                *[dma] * 12,
+                dma,
+                dma,
+                dma((FIRST,)),
+                dma((FIRST,)),
+                *[dma] * 8,
                 dma((5,)),
                 dma((5,)),
                 pltpu.SemaphoreType.REGULAR,

time: 113 us -> 113 us (level)
  no operation moved by 1% of the time
where the time goes in v5:
time: 113 us
  Pallas kernels  112 us (99%)
    pallas_call x1, Pallas kernels, shards(): pl.pallas_call(functools.partial(kernel, experts, rows), out_shape=shapes...  110 us

profile of v5, /device:TPU:65, one launch (start us, length us, event | category | flops | bytes accessed | tf_op | source)
XLA Modules:
  0.0 112.7 jit_solution(6549236749227428877)
XLA Ops:
  0.6 109.9 %serve.1 = (bf16[16,64,2048]{2,1,0:T(8,128)(2,1)S(1)}, f32[16,64]{1,0:T(8,128)S(1)}, bf16[64,2048]{1,0:T(8,128)(2,1)S(1)}) custom-call(f32[16,1024,128]{2,1,0:T(8,128)} %w_hbm.1, f32[16,128]{1,0:T(8,128)} %bitcast.3, f32[1,128]{1,0:T(1,128)} %bitcast.4), custom_call_target="tpu_custom_call" | custom-call | tf_op jit(solution)/shard_map/serve/pallas_call | solution.py:409
  110.5 2.1 %place.1 = (bf16[16,64,2048]{2,1,0:T(8,128)(2,1)}, f32[16,64]{1,0:T(8,128)}, bf16[64,2048]{1,0:T(8,128)(2,1)}) custom-call(bf16[16,64,2048]{2,1,0:T(8,128)(2,1)S(1)} %get-tuple-element.9.final_in, f32[16,64]{1,0:T(8,128)S(1)} %get-tuple-element.10.scale_in, bf16[64,2048]{1,0:T(8,128)(2,1)S(1)} %get-tuple-element.11.router_in), custom_call_target="tpu_custom_call" | custom-call | tf_op jit(solution)/shard_map/place/pallas_call | solution.py:448
